TPU v7x, 32 devices: a whole 2x2x4 slice. The times are simulated.
32 devices in a mesh: ep: 4 (over y, x), fsdp: 8 (over z, core).
Axes of the slice: x: 2, y: 2, z: 4, core: 2. Of those that a mesh axis runs over, the one named last changes fastest.
Arguments:
- train_gate: float32 [64, 2048, 1408], P('ep', 'fsdp'), may hold values from -0.1875 to 0.1875
- other_gate: bfloat16 [64, 2048, 1408], P('ep', 'fsdp'), may hold values from -0.0625 to 0.0625
- train_up: float32 [64, 2048, 1408], P('ep', 'fsdp'), may hold values from -0.1875 to 0.1875
- other_up: bfloat16 [64, 2048, 1408], P('ep', 'fsdp'), may hold values from -0.0625 to 0.0625
- router_weight: float32 [2048, 64], P('fsdp', 'ep'), may hold values from -0.125 to 0.125
- router_gain: float32 [2048], P('fsdp'), may hold values from 0.25 to 1.75
Outputs:
- ready_gate: bfloat16 [64, 2048, 1408], P('ep', None, 'fsdp')
- ready_up: bfloat16 [64, 2048, 1408], P('ep', None, 'fsdp')
- scale_gate: float32 [64, 1408], P('ep', 'fsdp')
- scale_up: float32 [64, 1408], P('ep', 'fsdp')
- serve_router: bfloat16 [2048, 64], replicated
All inputs are finite; a program needn't handle non-finite values. Where the computation divides by a largest or mean magnitude, that divisor is 1e-20 or more.
Results may differ from a plain program's by a relative error of at most 0.001.
Values may be sent and summed in bfloat16 or wider, within the bound.
No kernel may reach another device: no remote copies, remote signals or barrier semaphores. Data moves between devices by JAX's collectives and lax.ppermute only.
A program may use at most 192 MiB of HBM per device.

v0:
```python
import jax
import jax.numpy as jnp
from jax import lax
from jax.sharding import PartitionSpec as P


def per_device(train_gate, other_gate, train_up, other_up, router_weight, router_gain):
    latest_gate = train_gate + other_gate.astype(jnp.float32)
    latest_up = train_up + other_up.astype(jnp.float32)
    scale_gate, scale_up = lax.pmax(
        (jnp.max(jnp.abs(latest_gate), axis=1), jnp.max(jnp.abs(latest_up), axis=1)), "fsdp"
    )
    narrow_gate, narrow_up = (
        (latest_gate / jnp.expand_dims(scale_gate, 1)).astype(jnp.bfloat16),
        (latest_up / jnp.expand_dims(scale_up, 1)).astype(jnp.bfloat16),
    )
    ready_gate, ready_up = (
        lax.all_to_all(narrow_gate, "fsdp", split_axis=2, concat_axis=1, tiled=True),
        lax.all_to_all(narrow_up, "fsdp", split_axis=2, concat_axis=1, tiled=True),
    )
    scale_gate = lax.dynamic_slice_in_dim(
        scale_gate, lax.axis_index("fsdp") * ready_gate.shape[2], ready_gate.shape[2], axis=1
    )
    scale_up = lax.dynamic_slice_in_dim(
        scale_up, lax.axis_index("fsdp") * ready_up.shape[2], ready_up.shape[2], axis=1
    )
    part_router = (router_weight * router_gain[:, None]).astype(jnp.bfloat16)
    row_router = lax.all_gather(part_router, "fsdp", axis=0, tiled=True)
    serve_router = lax.all_gather(row_router, "ep", axis=1, tiled=True)
    return (ready_gate, ready_up, scale_gate, scale_up, serve_router)


def solution(mesh):
    in_specs = (
        P("ep", "fsdp", None),
        P("ep", "fsdp", None),
        P("ep", "fsdp", None),
        P("ep", "fsdp", None),
        P("fsdp", "ep"),
        P("fsdp"),
    )
    out_specs = (
        P("ep", None, "fsdp"),
        P("ep", None, "fsdp"),
        P("ep", "fsdp"),
        P("ep", "fsdp"),
        P(),
    )
    return jax.shard_map(
        per_device, mesh=mesh, in_specs=in_specs, out_specs=out_specs, check_vma=False
    )
```

profile of v0, /device:TPU:0, one launch (start us, length us, event | category | flops | bytes accessed | tf_op | source)
XLA Modules:
  0.0 809.5 jit_solution(1631548331659294860)
XLA Ops:
  7.2 0.0 all-reduce.3.cloned.1.call-start
  7.2 23.7 %copy.38 = f32[16,256,1408]{1,0,2:T(8,128)} copy(f32[16,256,1408]{2,1,0:T(8,128)} %param.8) | data formatting | bytes 46137344 | tf_op args[2]
  30.9 16.4 %copy.37 = bf16[16,256,1408]{1,0,2:T(8,128)(2,1)} copy(bf16[16,256,1408]{2,1,0:T(8,128)(2,1)} %param.9) | data formatting | bytes 23068672 | tf_op args[3]
  47.2 23.7 %copy.34 = f32[16,256,1408]{1,0,2:T(8,128)} copy(f32[16,256,1408]{2,1,0:T(8,128)} %param.6) | data formatting | bytes 46137344 | tf_op args[0]
  70.9 16.4 %copy.33 = bf16[16,256,1408]{1,0,2:T(8,128)(2,1)} copy(bf16[16,256,1408]{2,1,0:T(8,128)(2,1)} %param.7) | data formatting | bytes 23068672 | tf_op args[1]
  87.3 0.0 copy-start
  87.3 0.0 copy-start.1
  87.3 20.8 %abs_reduce_fusion = f32[16,1408]{0,1:T(8,128)} fusion(f32[16,256,1408]{1,0,2:T(8,128)} %copy.38, bf16[16,256,1408]{1,0,2:T(8,128)(2,1)} %copy.37), kind=kLoop, calls=%fused_computation.1 | loop fusion | flops 23046144 | bytes 34693120 | tf_op jit(solution)/shard_map/reduce_max | solution.py:11
  108.1 0.0 copy-done
  108.1 0.0 copy-done.1
  108.1 14.9 %abs_reduce_fusion.1 = f32[16,1408]{0,1:T(8,128)} fusion(f32[16,256,1408]{1,0,2:T(8,128)S(1)} %copy-done, bf16[16,256,1408]{1,0,2:T(8,128)(2,1)S(1)} %copy-done.1), kind=kLoop, calls=%fused_computation.4 | loop fusion | flops 23046144 | bytes 34693120 | tf_op jit(solution)/shard_map/reduce_max | solution.py:11
  123.0 0.0 all-reduce.3.cloned.1.call-update
  123.0 64.1 %all-reduce.3.cloned.1.call-done = (f32[16,1408]{0,1:T(8,128)}, f32[16,1408]{0,1:T(8,128)}) async-done(((f32[16,1408]{0,1:T(8,128)}, f32[16,1408]{0,1:T(8,128)}), (f32[16,1408]{0,1:T(8,128)}, f32[16,1408]{0,1:T(8,128)})) %all-reduce.3.cloned.1.call-update) | async-done | bytes 180240 | tf_op jit(solution)/shard_map/pmax | solution.py:10
  187.2 27.3 %divide_convert_fusion = (bf16[16,256,1408]{1,0,2:T(8,128)(2,1)}, bf16[16,256,1408]{1,0,2:T(8,128)(2,1)S(1)}) fusion(f32[16,256,1408]{1,0,2:T(8,128)} %copy.38, bf16[16,256,1408]{1,0,2:T(8,128)(2,1)} %copy.37, f32[16,1408]{0,1:T(8,128)} %get-tuple-element.11, f32[16,1408]{0,1:T(8,128)} %get-tuple-element.10, f32[16,256,1408]{1,0,2:T(8,128)} %copy.34, ...), kind=kLoop, calls=%fused_computation | loop fusion | flops 46137344 | bytes 92454912 | tf_op jit(solution)/shard_map/convert_element_type | solution.py:15
  214.5 0.0 copy-start.2
  214.5 0.0 copy-start.3
  214.5 255.0 %all_to_all.36 = bf16[16,256,1408]{1,0,2:T(8,128)(2,1)} all-to-all(bf16[16,256,1408]{1,0,2:T(8,128)(2,1)S(1)} %get-tuple-element.13), channel_id=1, replica_groups=mesh['ep'=4,'fsdp'=8] {'fsdp'}, dimensions={2} | all-to-all | bytes 23068672 | tf_op jit(solution)/shard_map/all_to_all | solution.py:18
  469.5 5.3 all-to-all-start.1
  474.8 0.0 copy-done.2
  474.8 0.0 copy-done.3
  474.8 257.3 %all_gather.6 = bf16[2048,16]{0,1:T(8,128)(2,1)S(1)} all-gather(bf16[256,16]{0,1:T(8,128)(2,1)S(1)} %multiply_convert_fusion), channel_id=1, replica_groups=mesh['ep'=4,'fsdp'=8] {'fsdp'}, dimensions={0}, use_global_device_ids=true | all-gather | bytes 73728 | tf_op jit(solution)/shard_map/all_gather | solution.py:28
  732.1 8.9 %all_gather.7 = bf16[2048,64]{0,1:T(8,128)(2,1)S(1)} all-gather(bf16[2048,16]{0,1:T(8,128)(2,1)S(1)} %all_gather.6), channel_id=1, replica_groups=mesh['ep'=4,'fsdp'=8] {'ep'}, dimensions={1}, use_global_device_ids=true | all-gather | bytes 327680 | tf_op jit(solution)/shard_map/all_gather | solution.py:29
  741.0 0.9 constant_dynamic-slice_fusion
  742.0 0.7 copy.41
  742.6 0.7 copy.42
  743.3 11.3 %copy.36 = bf16[16,8,256,176]{2,1,3,0:T(8,128)(2,1)} copy(bf16[16,8,256,176]{2,0,3,1:T(8,128)(2,1)} %bitcast.14) | data formatting | bytes 23068672 | tf_op jit(solution)/shard_map/all_to_all | solution.py:18
  754.7 18.0 %all_to_all.29 = bf16[16,2048,176]{1,2,0:T(8,128)(2,1)} reshape(bf16[16,8,256,176]{2,1,3,0:T(8,128)(2,1)} %copy.36) | data formatting | bytes 23068672 | tf_op jit(solution)/shard_map/all_to_all | solution.py:18
  772.6 0.0 all-to-all-done.1
  772.6 11.4 %copy.40 = bf16[16,8,256,176]{2,1,3,0:T(8,128)(2,1)} copy(bf16[16,8,256,176]{2,0,3,1:T(8,128)(2,1)} %bitcast.5) | data formatting | bytes 23068672 | tf_op jit(solution)/shard_map/all_to_all | solution.py:19
  784.0 18.0 %all_to_all.33 = bf16[16,2048,176]{1,2,0:T(8,128)(2,1)} reshape(bf16[16,8,256,176]{2,1,3,0:T(8,128)(2,1)} %copy.40) | data formatting | bytes 23068672 | tf_op jit(solution)/shard_map/all_to_all | solution.py:19
  802.0 0.7 copy.48
  (1 shorter events, 0.0 us)
Async XLA Ops:
  7.2 180.0 %all-reduce.3.cloned.1.call-start = ((), (), s32[]{:S(2)}) async-start(), calls=%async_computation.2 | async-start | bytes 2883584 | tf_op jit(solution)/shard_map/pmax | solution.py:10
  87.3 20.8 %copy-start = (f32[16,256,1408]{1,0,2:T(8,128)S(1)}, f32[16,256,1408]{1,0,2:T(8,128)}, u32[]{:S(2)}) copy-start(f32[16,256,1408]{1,0,2:T(8,128)} %copy.34) | copy-start | bytes 69206016
  87.3 20.9 %copy-start.1 = (bf16[16,256,1408]{1,0,2:T(8,128)(2,1)S(1)}, bf16[16,256,1408]{1,0,2:T(8,128)(2,1)}, u32[]{:S(2)}) copy-start(bf16[16,256,1408]{1,0,2:T(8,128)(2,1)} %copy.33) | copy-start | bytes 34603012
  214.5 260.3 %copy-start.2 = (f32[256,16]{0,1:T(8,128)S(1)}, f32[256,16]{0,1:T(8,128)}, u32[]{:S(2)}) copy-start(f32[256,16]{0,1:T(8,128)} %param.10) | copy-start | bytes 49156
  214.5 260.3 %copy-start.3 = (f32[256]{0:T(256)S(1)}, f32[256]{0:T(256)}, u32[]{:S(2)}) copy-start(f32[256]{0:T(256)} %param.11) | copy-start | bytes 3076
  469.5 303.1 %all-to-all-start.1 = ((bf16[16,256,1408]{1,0,2:T(8,128)(2,1)}), bf16[16,256,1408]{1,0,2:T(8,128)(2,1)}, u32[]{:S(2)}, u32[]{:S(2)}) async-start(bf16[16,256,1408]{1,0,2:T(8,128)(2,1)} %get-tuple-element.12), calls=%async_computation.1 | async-start | bytes 23068672 | tf_op jit(solution)/shard_map/all_to_all | solution.py:19
Sparse Core Ops, SparseCore 0:
  123.2 63.9 all-reduce.2
where the time goes:
time: 812 us; the launch traced here: 810 us
  blocking collectives  521 us (64%)
  local copies, waits for them, and re-layouts  142 us (17%)
  waiting for transfers between devices  64.2 us (8%)
  other arithmetic  63 us (8%)
  between operations  14.1 us (2%)
    all_gather x1, blocking collectives, per_device(): row_router = lax.all_gather(part_router, 'fsdp', axis=0, tiled=True)  257 us
    all_to_all x1, blocking collectives, per_device(): lax.all_to_all(narrow_gate, 'fsdp', split_axis=2, concat_axis=1, tiled=True)  255 us
    unnamed x15, local copies, waits for them, and re-layouts  82.2 us
    pmax x1, waiting for transfers between devices, per_device(): lax.pmax((jnp.max(jnp.abs(latest_gate), axis=1), jnp.max(jnp.abs(latest_u...  64.1 us
    all_to_all x2, local copies, waits for them, and re-layouts, per_device(): lax.all_to_all(narrow_up, 'fsdp', split_axis=2, concat_axis=1, tiled=True)  29.3 us
    all_to_all x2, local copies, waits for them, and re-layouts, per_device(): lax.all_to_all(narrow_gate, 'fsdp', split_axis=2, concat_axis=1, tiled=True)  29.3 us
    convert_element_type x1, other arithmetic, per_device(): (latest_up / jnp.expand_dims(scale_up, 1)).astype(jnp.bfloat16)  27.3 us
    reduce_max x1, other arithmetic, per_device(): jnp.max(jnp.abs(latest_up), axis=1)  20.8 us
  transfers between devices with their start and end apart: 2, of which 1 were waited for; matrix products, arithmetic and copies ran while one was open for 2% of the time, Pallas kernels for 0%

commit v1 on v0

--- a/solution.py
+++ b/solution.py
@@ -15,7 +15,12 @@
         (latest_up / jnp.expand_dims(scale_up, 1)).astype(jnp.bfloat16),
     )
     ready_gate, ready_up = (
-        lax.all_to_all(narrow_gate, "fsdp", split_axis=2, concat_axis=1, tiled=True),
+        jnp.concatenate(
+            lax.all_to_all(
+                jnp.stack(jnp.split(narrow_gate, lax.axis_size("fsdp"), axis=2)), "fsdp", 0, 0
+            ),
+            axis=1,
+        ),
         lax.all_to_all(narrow_up, "fsdp", split_axis=2, concat_axis=1, tiled=True),
     )
     scale_gate = lax.dynamic_slice_in_dim(

time: 812 us -> 776 us (0.956)
  blocking collectives: 521 us -> 266 us
  waiting for transfers between devices: 64.2 us -> 295 us
  local copies, waits for them, and re-layouts: 142 us -> 130 us
    all_to_all x1 -> x0, blocking collectives: 255 us -> none  [per_device(): lax.all_to_all(narrow_gate, 'fsdp', split_axis=2, concat_axis=1, tiled=True)]
    all_to_all x0 -> x1, waiting for transfers between devices: none -> 235 us  [per_device(): lax.all_to_all(jnp.stack(jnp.split(narrow_gate, lax.axis_size('fsdp'), ax...]
    all_to_all x2 -> x0, local copies, waits for them, and re-layouts: 29.3 us -> none  [per_device(): lax.all_to_all(narrow_gate, 'fsdp', split_axis=2, concat_axis=1, tiled=True)]
    convert_element_type x0 -> x1, other arithmetic: none -> 12 us  [per_device(): (latest_gate / jnp.expand_dims(scale_gate, 1)).astype(jnp.bfloat16)]
    convert_element_type x1, other arithmetic: 27.3 us -> 16.6 us  [per_device(): (latest_up / jnp.expand_dims(scale_up, 1)).astype(jnp.bfloat16)]
    reshape x0 -> x1, local copies, waits for them, and re-layouts: none -> 10 us  [per_device(): jnp.concatenate(lax.all_to_all(jnp.stack(jnp.split(narrow_gate, lax.axis_...]
    unnamed x15 -> x23, local copies, waits for them, and re-layouts: 82.2 us -> 88.1 us
  transfers between devices with their start and end apart: 2 -> 3, of which waited for: 1 -> 2; matrix products, arithmetic and copies ran while one was open for 2% -> 4% of each run, Pallas kernels for 0% -> 0%
where the time goes in v1:
time: 776 us; the launch traced here: 773 us
  waiting for transfers between devices  295 us (38%)
  blocking collectives  266 us (34%)
  local copies, waits for them, and re-layouts  130 us (17%)
  other arithmetic  57.4 us (7%)
  between operations  14.1 us (2%)
  starting transfers between devices  10.7 us (1%)
    all_gather x1, blocking collectives, per_device(): row_router = lax.all_gather(part_router, 'fsdp', axis=0, tiled=True)  257 us
    all_to_all x1, waiting for transfers between devices, per_device(): lax.all_to_all(jnp.stack(jnp.split(narrow_gate, lax.axis_size('fsdp'), ax...  235 us
    unnamed x23, local copies, waits for them, and re-layouts  88.1 us
    pmax x1, waiting for transfers between devices, per_device(): lax.pmax((jnp.max(jnp.abs(latest_gate), axis=1), jnp.max(jnp.abs(latest_u...  60.2 us
    all_to_all x2, local copies, waits for them, and re-layouts, per_device(): lax.all_to_all(narrow_up, 'fsdp', split_axis=2, concat_axis=1, tiled=True)  29.3 us
    reduce_max x1, other arithmetic, per_device(): jnp.max(jnp.abs(latest_up), axis=1)  20.8 us
    convert_element_type x1, other arithmetic, per_device(): (latest_up / jnp.expand_dims(scale_up, 1)).astype(jnp.bfloat16)  16.6 us
  transfers between devices with their start and end apart: 3, of which 2 were waited for; matrix products, arithmetic and copies ran while one was open for 4% of the time, Pallas kernels for 0%

profile of v1, /device:TPU:0, one launch (start us, length us, event | category | flops | bytes accessed | tf_op | source)
XLA Modules:
  0.0 773.4 jit_solution(17048523216744664075)
XLA Ops:
  7.2 0.0 all-reduce.3.cloned.1.call-start
  7.2 23.7 %copy.39 = f32[16,256,1408]{1,0,2:T(8,128)} copy(f32[16,256,1408]{2,1,0:T(8,128)} %param.8) | data formatting | bytes 46137344 | tf_op args[2]
  30.9 16.4 %copy.38 = bf16[16,256,1408]{1,0,2:T(8,128)(2,1)} copy(bf16[16,256,1408]{2,1,0:T(8,128)(2,1)} %param.9) | data formatting | bytes 23068672 | tf_op args[3]
  47.2 23.3 %copy.36 = f32[16,256,1408]{1,2,0:T(8,128)} copy(f32[16,256,1408]{2,1,0:T(8,128)} %param.6) | data formatting | bytes 46137344 | tf_op args[0]
  70.5 15.0 %copy.35 = bf16[16,256,1408]{1,2,0:T(8,128)(2,1)} copy(bf16[16,256,1408]{2,1,0:T(8,128)(2,1)} %param.7) | data formatting | bytes 23068672 | tf_op args[1]
  85.5 20.8 %abs_reduce_fusion = f32[16,1408]{0,1:T(8,128)} fusion(f32[16,256,1408]{1,0,2:T(8,128)} %copy.39, bf16[16,256,1408]{1,0,2:T(8,128)(2,1)} %copy.38), kind=kLoop, calls=%fused_computation.1 | loop fusion | flops 23046144 | bytes 34693120 | tf_op jit(solution)/shard_map/reduce_max | solution.py:11
  106.4 0.0 copy-done.1
  106.4 7.9 %abs_reduce_fusion.1 = f32[16,1408]{1,0:T(8,128)} fusion(f32[16,256,1408]{1,2,0:T(8,128)S(1)} %copy-done, bf16[16,256,1408]{1,2,0:T(8,128)(2,1)S(1)} %copy-done.1), kind=kLoop, calls=%fused_computation.4 | loop fusion | flops 23046144 | bytes 34693120 | tf_op jit(solution)/shard_map/reduce_max | solution.py:11
  114.3 0.0 all-reduce.3.cloned.1.call-update
  114.3 60.2 %all-reduce.3.cloned.1.call-done = (f32[16,1408]{1,0:T(8,128)}, f32[16,1408]{0,1:T(8,128)}) async-done(((f32[16,1408]{1,0:T(8,128)}, f32[16,1408]{0,1:T(8,128)}), (f32[16,1408]{1,0:T(8,128)}, f32[16,1408]{0,1:T(8,128)})) %all-reduce.3.cloned.1.call-update) | async-done | bytes 180240 | tf_op jit(solution)/shard_map/pmax | solution.py:10
  174.5 12.0 %divide_convert_fusion.1 = bf16[16,256,1408]{1,2,0:T(8,128)(2,1)S(1)} fusion(f32[16,256,1408]{1,2,0:T(8,128)} %copy.36, bf16[16,256,1408]{1,2,0:T(8,128)(2,1)} %copy.35, f32[16,1408]{1,0:T(8,128)} %get-tuple-element.10), kind=kLoop, calls=%fused_computation.3 | loop fusion | flops 23068672 | bytes 46227456 | tf_op jit(solution)/shard_map/convert_element_type | solution.py:14
  186.6 1.2 fusion.7
  187.8 1.2 fusion.6
  189.0 1.2 fusion.5
  190.2 1.2 fusion.4
  191.4 1.2 fusion.3
  192.6 1.2 fusion.2
  193.8 1.2 fusion.1
  195.0 1.2 fusion
  196.2 5.4 all-to-all-start
  201.6 16.6 %divide_convert_fusion = bf16[16,256,1408]{1,0,2:T(8,128)(2,1)} fusion(f32[16,256,1408]{1,0,2:T(8,128)} %copy.39, bf16[16,256,1408]{1,0,2:T(8,128)(2,1)} %copy.38, f32[16,1408]{0,1:T(8,128)S(1)} %copy-done.2), kind=kLoop, calls=%fused_computation | loop fusion | flops 23068672 | bytes 46227456 | tf_op jit(solution)/shard_map/convert_element_type | solution.py:15
  218.2 234.6 %all-to-all-done = bf16[8,16,256,176]{2,3,1,0:T(8,128)(2,1)} async-done(((bf16[8,16,256,176]{2,3,1,0:T(8,128)(2,1)}), bf16[8,16,256,176]{2,3,1,0:T(8,128)(2,1)}, u32[]{:S(2)}, u32[]{:S(2)}) %all-to-all-start) | async-done | bytes 11534368 | tf_op jit(solution)/shard_map/all_to_all | solution.py:19
  452.8 5.3 all-to-all-start.1
  458.1 257.3 %all_gather.6 = bf16[2048,16]{0,1:T(8,128)(2,1)S(1)} all-gather(bf16[256,16]{0,1:T(8,128)(2,1)S(1)} %multiply_convert_fusion), channel_id=1, replica_groups=mesh['ep'=4,'fsdp'=8] {'fsdp'}, dimensions={0}, use_global_device_ids=true | all-gather | bytes 73728 | tf_op jit(solution)/shard_map/all_gather | solution.py:33
  715.4 8.9 %all_gather.7 = bf16[2048,64]{0,1:T(8,128)(2,1)S(1)} all-gather(bf16[2048,16]{0,1:T(8,128)(2,1)S(1)} %all_gather.6), channel_id=1, replica_groups=mesh['ep'=4,'fsdp'=8] {'ep'}, dimensions={1}, use_global_device_ids=true | all-gather | bytes 327680 | tf_op jit(solution)/shard_map/all_gather | solution.py:34
  724.4 0.7 copy.42
  725.0 1.4 constant_dynamic-slice_fusion.1
  726.5 10.0 %copy.44 = bf16[8,16,22,8,256]{4,3,0,2,1:T(8,128)(2,1)} copy(bf16[8,16,22,8,256]{4,3,2,1,0:T(8,128)(2,1)} %bitcast.12) | data formatting | bytes 23068672 | tf_op jit(solution)/shard_map/reshape | solution.py:18
  736.5 0.0 all-to-all-done.1
  736.5 11.4 %copy.41 = bf16[16,8,256,176]{2,1,3,0:T(8,128)(2,1)} copy(bf16[16,8,256,176]{2,0,3,1:T(8,128)(2,1)} %bitcast.11) | data formatting | bytes 23068672 | tf_op jit(solution)/shard_map/all_to_all | solution.py:24
  747.8 18.0 %all_to_all.20 = bf16[16,2048,176]{1,2,0:T(8,128)(2,1)} reshape(bf16[16,8,256,176]{2,1,3,0:T(8,128)(2,1)} %copy.41) | data formatting | bytes 23068672 | tf_op jit(solution)/shard_map/all_to_all | solution.py:24
  765.8 0.7 copy.55
  (11 shorter events, 0.0 us)
Async XLA Ops:
  7.2 167.4 %all-reduce.3.cloned.1.call-start = ((), (), s32[]{:S(2)}) async-start(), calls=%async_computation.2 | async-start | bytes 1622016 | tf_op jit(solution)/shard_map/pmax | solution.py:10
  85.5 20.9 %copy-start = (f32[16,256,1408]{1,2,0:T(8,128)S(1)}, f32[16,256,1408]{1,2,0:T(8,128)}, u32[]{:S(2)}) copy-start(f32[16,256,1408]{1,2,0:T(8,128)} %copy.36) | copy-start | bytes 69206016
  85.5 20.9 %copy-start.1 = (bf16[16,256,1408]{1,2,0:T(8,128)(2,1)S(1)}, bf16[16,256,1408]{1,2,0:T(8,128)(2,1)}, u32[]{:S(2)}) copy-start(bf16[16,256,1408]{1,2,0:T(8,128)(2,1)} %copy.35) | copy-start | bytes 34603012
  196.2 5.4 copy-start.2
  196.2 256.7 %all-to-all-start = ((bf16[8,16,256,176]{2,3,1,0:T(8,128)(2,1)}), bf16[8,16,256,176]{2,3,1,0:T(8,128)(2,1)}, u32[]{:S(2)}, u32[]{:S(2)}) async-start(bf16[8,16,256,176]{2,3,1,0:T(8,128)(2,1)} %fusion), calls=%async_computation | async-start | bytes 23068672 | tf_op jit(solution)/shard_map/all_to_all | solution.py:19
  218.2 239.9 %copy-start.3 = (f32[256,16]{0,1:T(8,128)S(1)}, f32[256,16]{0,1:T(8,128)}, u32[]{:S(2)}) copy-start(f32[256,16]{0,1:T(8,128)} %param.10) | copy-start | bytes 49156
  218.2 239.9 %copy-start.4 = (f32[256]{0:T(256)S(1)}, f32[256]{0:T(256)}, u32[]{:S(2)}) copy-start(f32[256]{0:T(256)} %param.11) | copy-start | bytes 3076
  452.8 283.6 %all-to-all-start.1 = ((bf16[16,256,1408]{1,0,2:T(8,128)(2,1)}), bf16[16,256,1408]{1,0,2:T(8,128)(2,1)}, u32[]{:S(2)}, u32[]{:S(2)}) async-start(bf16[16,256,1408]{1,0,2:T(8,128)(2,1)} %divide_convert_fusion), calls=%async_computation.1 | async-start | bytes 23068672 | tf_op jit(solution)/shard_map/all_to_all | solution.py:24
Sparse Core Ops, SparseCore 0:
  114.4 60.0 all-reduce.2
